TPU v7x, 32 devices: a whole 2x2x4 slice. The times are simulated.
32 devices in a mesh: dom: 8 (over y, x, core), feat: 4 (over z).
Axes of the slice: x: 2, y: 2, z: 4, core: 2. Of those that a mesh axis runs over, the one named last changes fastest.
Arguments:
- features: bfloat16 [512, 65536], P('feat', 'dom'), may hold values from -3 to 3
- send_blocks: int32 [8, 8, 8], P('dom'), may hold values from 0 to 63, as said below
- counts: int32 [8, 8], P('dom'), may hold values from 0 to 8, as said below
- tile_blocks: int32 [24, 512], P(None, 'dom'), may hold values from 0 to 127, as said below
- neighbours: int32 [24, 65536], P(None, 'dom'), may hold values from 0 to 127
- degree: int32 [65536], P('dom'), may hold values from 1 to 24
- epsilon: float32 [1], replicated, may hold values from -0.3 to 0.6
- w_first: bfloat16 [512, 512], replicated, may hold values from -0.25 to 0.25
- b_first: float32 [512], replicated, may hold values from -3 to 3
- w_second: bfloat16 [512, 512], replicated, may hold values from -0.25 to 0.25
- b_second: float32 [512], replicated, may hold values from -3 to 3
Outputs:
- updated: bfloat16 [65536, 512], P(('dom', 'feat'))
Inputs may be any that keep to these rules, and one draw needn't show every extreme that they name: `send_blocks`: entry [q, p, s] is a row block of partition q; the entries of one pair (q, p) are distinct. counts[q, p] leading slots of send_blocks[q, p] are used; zero where q == p; in every draw some partition receives 8 blocks from every other partition. `tile_blocks`: an entry for a row block of partition p is below 64 (a row block of p) or equals 64 + q * 8 + s for a slot s of a partition q other than p.
All inputs are finite; a program needn't handle non-finite values.
Results may differ from a plain program's by a relative error of at most 0.0055.
Values may be sent and summed in bfloat16 or wider, within the bound.
No kernel may reach another device: no remote copies, remote signals or barrier semaphores. Data moves between devices by JAX's collectives and lax.ppermute only.
A program may use at most 64 MiB of HBM per device.

v0:
```python
import functools

import jax
import jax.numpy as jnp
from jax import lax
from jax.experimental import pallas as pl
from jax.experimental.pallas import tpu as pltpu
from jax.sharding import PartitionSpec as P


BLOCK = 128
PACK = 16

VMEM = pl.BlockSpec(memory_space=pltpu.VMEM)
SMEM = pl.BlockSpec(memory_space=pltpu.SMEM)


def exchange_order(size):
    return sorted(range(size), key=lambda s: (-s.bit_length(), s))


def column_parts(cols):
    first = cols * 3 // 8 // PACK * PACK
    return (0, first), (first, cols)


def pick_kernel(pos_ref, blocks_ref, counts_ref, feat_ref, *out_refs, slots):
    me = pos_ref[0]
    for i, out_ref in enumerate(out_refs):
        peer = jnp.bitwise_xor(me, i + 1)
        count = counts_ref[peer]
        for s in range(slots):
            start = pl.multiple_of(blocks_ref[peer, s] * BLOCK, BLOCK)
            tile = feat_ref[:, pl.ds(start, BLOCK)]
            out_ref[:, s * BLOCK : (s + 1) * BLOCK] = jnp.where(
                s < count, tile, jnp.zeros_like(tile)
            )


def gather_kernel(owner_ref, tiles_ref, gain_ref, near_ref, feat_ref, *rest, slots):
    halo_refs, out_ref, table_ref = rest[:-2], rest[-2], rest[-1]
    own = feat_ref.shape[1] // BLOCK
    width = near_ref.shape[0]
    chunk = out_ref.shape[1] // BLOCK
    for b in range(own):
        table_ref[b] = feat_ref[:, b * BLOCK : (b + 1) * BLOCK]
    for i, ref in enumerate(halo_refs):
        for s in range(slots):
            table_ref[own + slots + i * slots + s] = ref[:, s * BLOCK : (s + 1) * BLOCK]
    first = owner_ref[0] * chunk
    gain = gain_ref[0]
    ids = lax.broadcasted_iota(jnp.int32, (BLOCK, BLOCK), 0).astype(jnp.float32)
    ids = ids.astype(jnp.bfloat16)
    one, zero = jnp.ones((), jnp.bfloat16), jnp.zeros((), jnp.bfloat16)
    per = next(k for k in (4, 2, 1) if chunk % k == 0)

    @pl.loop(0, chunk // per)
    def _(step):
        for k in range(per):
            b = step * per + k
            block = first + b
            lanes = pl.ds(pl.multiple_of(block * BLOCK, BLOCK), BLOCK)
            left, right = [], []
            for j in range(width):
                left.append(table_ref[tiles_ref[j, block]])
                row = jnp.broadcast_to(near_ref[j : j + 1, lanes], (PACK, BLOCK))
                row = jnp.concatenate([row.astype(jnp.bfloat16)] * (BLOCK // PACK), axis=0)
                right.append(jnp.where(row == ids, one, zero))
            near = jnp.dot(
                jnp.concatenate(left, axis=1),
                jnp.concatenate(right, axis=0),
                preferred_element_type=jnp.float32,
            )
            mixed = gain * table_ref[block].astype(jnp.float32) + near
            place = pl.ds(pl.multiple_of(b * BLOCK, BLOCK), BLOCK)
            out_ref[:, place] = mixed.astype(jnp.bfloat16)


def network_kernel(rows_ref, w_first_ref, b_first_ref, w_second_ref, b_second_ref, *rest):
    parcels, out_ref = rest[:-1], rest[-1]
    flat = jnp.concatenate([ref[...] for ref in parcels], axis=0)
    weights = jnp.concatenate(
        [
            w_first_ref[pl.ds(pl.multiple_of(rows_ref[i], PACK), ref.shape[0]), :]
            for i, ref in enumerate(parcels)
        ],
        axis=0,
    )
    pre_act = (
        lax.dot_general(flat, weights, (((0,), (0,)), ((), ())), preferred_element_type=jnp.float32)
        + b_first_ref[...]
    )
    activated = jnp.maximum(pre_act, 0.0).astype(jnp.bfloat16)
    out_ref[...] = (
        jnp.dot(activated, w_second_ref[...], preferred_element_type=jnp.float32) + b_second_ref[...]
    ).astype(jnp.bfloat16)


def per_device(
    features,
    send_blocks,
    counts,
    tile_blocks,
    neighbours,
    degree,
    epsilon,
    w_first,
    b_first,
    w_second,
    b_second,
):
    cols, rows = features.shape
    parts = lax.axis_size("dom")
    groups = lax.axis_size("feat")
    me = lax.axis_index("dom").astype(jnp.int32)
    zed = lax.axis_index("feat").astype(jnp.int32)
    slots = send_blocks.shape[2]
    width = neighbours.shape[0]
    own = rows // BLOCK
    owned = rows // groups

    halo, pieces = [], []
    for low, high in column_parts(cols):
        piece = lax.slice_in_dim(features, low, high, axis=0)
        picked = pl.pallas_call(
            functools.partial(pick_kernel, slots=slots),
            in_specs=[SMEM, SMEM, SMEM, VMEM],
            out_specs=[VMEM] * (parts - 1),
            out_shape=[jax.ShapeDtypeStruct((high - low, slots * BLOCK), jnp.bfloat16)]
            * (parts - 1),
            name="pick",
        )(me[None], send_blocks[0], counts[0], piece)
        pieces.append(piece)
        arrived = []
        for i in range(parts - 1):
            arrived.append(lax.ppermute(picked[i], "dom", [(k, k ^ (i + 1)) for k in range(parts)]))
        halo.append(arrived)

    remote = tile_blocks - own
    tiles = jnp.where(
        remote < 0,
        tile_blocks,
        own + jnp.bitwise_xor(remote // slots, me) * slots + remote % slots,
    )
    gain = 1.0 + epsilon
    entry = jnp.arange(width, dtype=jnp.int32)[:, None]
    near_rows = jnp.where(entry < degree[None, :], neighbours, -1).astype(jnp.float32)
    parcels, starts = [], []
    for h, (low, high) in enumerate(column_parts(cols)):
        piece, arrived = pieces[h], halo[h]
        for shift in exchange_order(groups):
            owner = jnp.bitwise_xor(zed, shift)
            at = owner[None]
            parcels.append(
                pl.pallas_call(
                    functools.partial(gather_kernel, slots=slots),
                    in_specs=[SMEM, SMEM, SMEM] + [VMEM] * (2 + parts - 1),
                    out_specs=VMEM,
                    out_shape=jax.ShapeDtypeStruct((high - low, owned), jnp.bfloat16),
                    scratch_shapes=[
                        pltpu.VMEM((own + slots * parts, high - low, BLOCK), jnp.bfloat16)
                    ],
                    name="aggregate",
                )(at, tiles, gain, near_rows, piece, *arrived)
            )
            starts.append(owner * cols + low)
            if shift:
                parcels[-1] = lax.ppermute(
                    parcels[-1], "feat", [(k, k ^ shift) for k in range(groups)]
                )
    step = min(owned, 256)
    hidden, wide = w_second.shape
    fixed = lambda i: (0, 0)
    return pl.pallas_call(
        network_kernel,
        grid=(owned // step,),
        in_specs=[
            SMEM,
            pl.BlockSpec(w_first.shape, fixed),
            pl.BlockSpec((1, hidden), fixed),
            pl.BlockSpec(w_second.shape, fixed),
            pl.BlockSpec((1, wide), fixed),
        ]
        + [pl.BlockSpec((p.shape[0], step), lambda i: (0, i)) for p in parcels],
        out_specs=pl.BlockSpec((step, wide), lambda i: (i, 0)),
        out_shape=jax.ShapeDtypeStruct((owned, wide), jnp.bfloat16),
        name="network",
    )(jnp.stack(starts), w_first, b_first[None, :], w_second, b_second[None, :], *parcels)


def solution(mesh):
    return jax.shard_map(
        per_device,
        mesh=mesh,
        in_specs=(
            P("feat", "dom"),
            P("dom", None, None),
            P("dom", None),
            P(None, "dom"),
            P(None, "dom"),
            P("dom"),
            P(),
            P(),
            P(),
            P(),
            P(),
        ),
        out_specs=P(("dom", "feat"), None),
        check_vma=False,
    )
```

profile of v0, /device:TPU:0, one launch (start us, length us, event | category | flops | bytes accessed | tf_op | source)
XLA Modules:
  0.0 112.3 jit_solution(13197321825685134846)
XLA Ops:
  0.0 2.2 %slice.6.feat_ref = bf16[48,8192]{1,0:T(8,128)(2,1)} slice(bf16[128,8192]{1,0:T(8,128)(2,1)} %param.11), slice={[0:48], [0:8192]} | slice | bytes 1572864 | tf_op jit(solution)/shard_map/slice | solution.py:124
  2.2 2.2 %pick.2 = (bf16[48,1024]{1,0:T(8,128)(2,1)}, bf16[48,1024]{1,0:T(8,128)(2,1)}, bf16[48,1024]{1,0:T(8,128)(2,1)}, bf16[48,1024]{1,0:T(8,128)(2,1)}, bf16[48,1024]...) custom-call(s32[1]{0:T(128)} %bitcast.11.pos_ref, s32[8,8]{1,0:T(8,128)} %bitcast.17, s32[8]{0:T(128)} %bitcast.21, ...), custom_call_target="tpu_custom_call" | custom-call | tf_op jit(solution)/shard_map/pick/pallas_call | solution.py:125
  4.5 0.0 copy-start.22
  4.5 0.6 collective-permute-start
  5.1 2.6 %collective-permute-start.1 = (bf16[48,1024]{1,0:T(8,128)(2,1)}, bf16[48,1024]{1,0:T(8,128)(2,1)S(1)}, u32[]{:S(2)}, u32[]{:S(2)}) collective-permute-start(bf16[48,1024]{1,0:T(8,128)(2,1)} %get-tuple-element.20), channel_id=1, source_target_pairs={{0,8},{4,12},{8,0},{12,4},{16,24},{20,28},{24,16},{28,20},{1,9},{5... | collective-permute-start | bytes 294920 | tf_op jit(solution)/shard_map/ppermute | solution.py:136
  7.6 0.0 collective-permute-start.2
  7.7 1.8 %collective-permute-start.3 = (bf16[48,1024]{1,0:T(8,128)(2,1)}, bf16[48,1024]{1,0:T(8,128)(2,1)S(1)}, u32[]{:S(2)}, u32[]{:S(2)}) collective-permute-start(bf16[48,1024]{1,0:T(8,128)(2,1)} %get-tuple-element.22), channel_id=1, source_target_pairs={{0,16},{4,20},{8,24},{12,28},{16,0},{20,4},{24,8},{28,12},{1,17},{... | collective-permute-start | bytes 294920 | tf_op jit(solution)/shard_map/ppermute | solution.py:136
  9.4 1.1 %slice.7.feat_ref = bf16[80,8192]{1,0:T(8,128)(2,1)} slice(bf16[128,8192]{1,0:T(8,128)(2,1)S(1)} %copy-done.7), slice={[48:128], [0:8192]} | slice | bytes 2621440 | tf_op jit(solution)/shard_map/slice | solution.py:124
  10.6 2.7 %pick.3 = (bf16[80,1024]{1,0:T(8,128)(2,1)}, bf16[80,1024]{1,0:T(8,128)(2,1)}, bf16[80,1024]{1,0:T(8,128)(2,1)}, bf16[80,1024]{1,0:T(8,128)(2,1)}, bf16[80,1024]...) custom-call(s32[1]{0:T(128)} %bitcast.11.pos_ref, s32[8,8]{1,0:T(8,128)} %bitcast.18, s32[8]{0:T(128)} %bitcast.22, ...), custom_call_target="tpu_custom_call" | custom-call | tf_op jit(solution)/shard_map/pick/pallas_call | solution.py:125
  13.2 0.1 collective-permute-start.10
  13.3 0.0 collective-permute-done.rest_0_
  13.3 1.5 %collective-permute-start.11 = (bf16[80,1024]{1,0:T(8,128)(2,1)}, bf16[80,1024]{1,0:T(8,128)(2,1)S(1)}, u32[]{:S(2)}, u32[]{:S(2)}) collective-permute-start(bf16[80,1024]{1,0:T(8,128)(2,1)} %get-tuple-element.27), channel_id=1, source_target_pairs={{0,8},{4,12},{8,0},{12,4},{16,24},{20,28},{24,16},{28,20},{1,9},{5... | collective-permute-start | bytes 491528 | tf_op jit(solution)/shard_map/ppermute | solution.py:136
  14.8 0.0 collective-permute-done.1.rest_1_
  14.8 0.3 collective-permute-start.4
  15.1 0.0 collective-permute-done.2.rest_2_
  15.1 1.6 %collective-permute-start.5 = (bf16[48,1024]{1,0:T(8,128)(2,1)S(1)}, bf16[48,1024]{1,0:T(8,128)(2,1)S(1)}, u32[]{:S(2)}, u32[]{:S(2)}) collective-permute-start(bf16[48,1024]{1,0:T(8,128)(2,1)S(1)} %copy-done.25), channel_id=1, source_target_pairs={{0,24},{4,28},{8,16},{12,20},{16,8},{20,12},{24,0},{28,4},{1,25},{... | collective-permute-start | bytes 294920 | tf_op jit(solution)/shard_map/ppermute | solution.py:136
  16.6 0.0 collective-permute-done.3.rest_3_
  16.7 1.2 %collective-permute-start.6 = (bf16[48,1024]{1,0:T(8,128)(2,1)S(1)}, bf16[48,1024]{1,0:T(8,128)(2,1)S(1)}, u32[]{:S(2)}, u32[]{:S(2)}) collective-permute-start(bf16[48,1024]{1,0:T(8,128)(2,1)S(1)} %copy-done.24), channel_id=1, source_target_pairs={{0,28},{4,24},{8,20},{12,16},{16,12},{20,8},{24,4},{28,0},{1,29},{... | collective-permute-start | bytes 294920 | tf_op jit(solution)/shard_map/ppermute | solution.py:136
  17.8 1.0 select_convert_fusion.near_ref
  18.8 1.6 %collective-permute-done.4.rest_4_ = bf16[48,1024]{1,0:T(8,128)(2,1)S(1)} collective-permute-done((bf16[48,1024]{1,0:T(8,128)(2,1)}, bf16[48,1024]{1,0:T(8,128)(2,1)S(1)}, u32[]{:S(2)}, u32[]{:S(2)}) %collective-permute-start.4) | collective-permute-done | bytes 98336 | tf_op jit(solution)/shard_map/ppermute | solution.py:136
  20.4 0.0 collective-permute-start.12
  20.4 2.1 %collective-permute-done.5.rest_5_ = bf16[48,1024]{1,0:T(8,128)(2,1)S(1)} collective-permute-done((bf16[48,1024]{1,0:T(8,128)(2,1)S(1)}, bf16[48,1024]{1,0:T(8,128)(2,1)S(1)}, u32[]{:S(2)}, u32[]{:S(2)}) %collective-permute-start.5) | collective-permute-done | bytes 98336 | tf_op jit(solution)/shard_map/ppermute | solution.py:136
  22.5 1.6 %collective-permute-start.13 = (bf16[80,1024]{1,0:T(8,128)(2,1)}, bf16[80,1024]{1,0:T(8,128)(2,1)S(1)}, u32[]{:S(2)}, u32[]{:S(2)}) collective-permute-start(bf16[80,1024]{1,0:T(8,128)(2,1)} %get-tuple-element.29), channel_id=1, source_target_pairs={{0,16},{4,20},{8,24},{12,28},{16,0},{20,4},{24,8},{28,12},{1,17},{... | collective-permute-start | bytes 491528 | tf_op jit(solution)/shard_map/ppermute | solution.py:136
  24.2 0.0 collective-permute-done.6.rest_6_
  24.2 1.7 %collective-permute-start.14 = (bf16[80,1024]{1,0:T(8,128)(2,1)}, bf16[80,1024]{1,0:T(8,128)(2,1)S(1)}, u32[]{:S(2)}, u32[]{:S(2)}) collective-permute-start(bf16[80,1024]{1,0:T(8,128)(2,1)} %get-tuple-element.30), channel_id=1, source_target_pairs={{0,20},{4,16},{8,28},{12,24},{16,4},{20,0},{24,12},{28,8},{1,21},{... | collective-permute-start | bytes 491528 | tf_op jit(solution)/shard_map/ppermute | solution.py:136
  25.9 0.0 collective-permute-done.10.rest_0_
  25.9 1.7 %collective-permute-start.15 = (bf16[80,1024]{1,0:T(8,128)(2,1)}, bf16[80,1024]{1,0:T(8,128)(2,1)S(1)}, u32[]{:S(2)}, u32[]{:S(2)}) collective-permute-start(bf16[80,1024]{1,0:T(8,128)(2,1)} %get-tuple-element.31), channel_id=1, source_target_pairs={{0,24},{4,28},{8,16},{12,20},{16,8},{20,12},{24,0},{28,4},{1,25},{... | collective-permute-start | bytes 491528 | tf_op jit(solution)/shard_map/ppermute | solution.py:136
  27.7 0.0 collective-permute-done.11.rest_1_
  27.7 0.0 collective-permute-start.16
  27.7 0.7 fusion.4.tiles_ref
  29.1 4.8 %aggregate.10 = bf16[48,2048]{1,0:T(8,128)(2,1)} custom-call(s32[1]{0:T(128)} %bitcast.15.owner_ref, s32[24,64]{1,0:T(8,128)} %fusion.4.tiles_ref, f32[1]{0:T(128)S(6)} %add.36.gain_ref, f32[24,8192]{1,0:T(8,128)} %select_convert_fusion.near_ref, bf16[48,8192]{1,0:T(8,128)(2,1)} %slice.6.feat_ref, bf16[48,1024]{1,0:T(8,128)(2,1)} %copy-done.8, ...), custom_call_target="tpu_custom_call" | custom-call | tf_op jit(solution)/shard_map/aggregate/pallas_call | solution.py:155
  33.8 0.0 collective-permute-done.12.rest_2_
  33.8 1.5 %collective-permute-start.9 = (bf16[48,2048]{1,0:T(8,128)(2,1)}, bf16[48,2048]{1,0:T(8,128)(2,1)S(1)}, u32[]{:S(2)}, u32[]{:S(2)}) collective-permute-start(bf16[48,2048]{1,0:T(8,128)(2,1)} %aggregate.10), channel_id=1, source_target_pairs={{0,1},{1,0},{2,3},{3,2},{4,5},{5,4},{6,7},{7,6},{8,9},{9,8},{10,11... | collective-permute-start | bytes 589832 | tf_op jit(solution)/shard_map/ppermute | solution.py:168
  35.3 0.0 collective-permute-done.13.rest_3_
  35.3 5.0 %collective-permute-done.14.rest_4_ = bf16[80,1024]{1,0:T(8,128)(2,1)S(1)} collective-permute-done((bf16[80,1024]{1,0:T(8,128)(2,1)}, bf16[80,1024]{1,0:T(8,128)(2,1)S(1)}, u32[]{:S(2)}, u32[]{:S(2)}) %collective-permute-start.14) | collective-permute-done | bytes 163872 | tf_op jit(solution)/shard_map/ppermute | solution.py:136
  40.4 0.0 collective-permute-done.15.rest_5_
  40.4 0.0 collective-permute-done.16.rest_6_
  40.4 0.6 copy-done.4
  41.0 0.1 copy-done.5
  41.1 0.7 copy-done.6
  41.8 5.8 %aggregate.14 = bf16[80,2048]{1,0:T(8,128)(2,1)} custom-call(s32[1]{0:T(128)} %bitcast.15.owner_ref, s32[24,64]{1,0:T(8,128)} %fusion.4.tiles_ref, f32[1]{0:T(128)S(6)} %add.36.gain_ref, f32[24,8192]{1,0:T(8,128)} %select_convert_fusion.near_ref, bf16[80,8192]{1,0:T(8,128)(2,1)} %slice.7.feat_ref, bf16[80,1024]{1,0:T(8,128)(2,1)} %copy-done, ...), custom_call_target="tpu_custom_call" | custom-call | tf_op jit(solution)/shard_map/aggregate/pallas_call | solution.py:155
  47.5 1.8 %collective-permute-start.19 = (bf16[80,2048]{1,0:T(8,128)(2,1)}, bf16[80,2048]{1,0:T(8,128)(2,1)S(1)}, u32[]{:S(2)}, u32[]{:S(2)}) collective-permute-start(bf16[80,2048]{1,0:T(8,128)(2,1)} %aggregate.14), channel_id=1, source_target_pairs={{0,1},{1,0},{2,3},{3,2},{4,5},{5,4},{6,7},{7,6},{8,9},{9,8},{10,11... | collective-permute-start | bytes 983048 | tf_op jit(solution)/shard_map/ppermute | solution.py:168
  49.3 5.7 %aggregate.13 = bf16[80,2048]{1,0:T(8,128)(2,1)} custom-call(s32[1]{0:T(128)} %bitcast.14.owner_ref, s32[24,64]{1,0:T(8,128)} %fusion.4.tiles_ref, f32[1]{0:T(128)S(6)} %add.36.gain_ref, f32[24,8192]{1,0:T(8,128)} %select_convert_fusion.near_ref, bf16[80,8192]{1,0:T(8,128)(2,1)} %slice.7.feat_ref, bf16[80,1024]{1,0:T(8,128)(2,1)} %copy-done, ...), custom_call_target="tpu_custom_call" | custom-call | tf_op jit(solution)/shard_map/aggregate/pallas_call | solution.py:155
  55.1 2.5 %collective-permute-start.18 = (bf16[80,2048]{1,0:T(8,128)(2,1)}, bf16[80,2048]{1,0:T(8,128)(2,1)S(1)}, u32[]{:S(2)}, u32[]{:S(2)}) collective-permute-start(bf16[80,2048]{1,0:T(8,128)(2,1)} %aggregate.13), channel_id=1, source_target_pairs={{0,3},{1,2},{2,1},{3,0},{4,7},{5,6},{6,5},{7,4},{8,11},{9,10},{10,... | collective-permute-start | bytes 983048 | tf_op jit(solution)/shard_map/ppermute | solution.py:168
  57.5 5.7 %aggregate.12 = bf16[80,2048]{1,0:T(8,128)(2,1)} custom-call(s32[1]{0:T(128)} %bitcast.10.owner_ref, s32[24,64]{1,0:T(8,128)} %fusion.4.tiles_ref, f32[1]{0:T(128)S(6)} %add.36.gain_ref, f32[24,8192]{1,0:T(8,128)} %select_convert_fusion.near_ref, bf16[80,8192]{1,0:T(8,128)(2,1)} %slice.7.feat_ref, bf16[80,1024]{1,0:T(8,128)(2,1)} %copy-done, ...), custom_call_target="tpu_custom_call" | custom-call | tf_op jit(solution)/shard_map/aggregate/pallas_call | solution.py:155
  63.3 0.1 collective-permute-start.17
  63.4 4.7 %aggregate.9 = bf16[48,2048]{1,0:T(8,128)(2,1)} custom-call(s32[1]{0:T(128)} %bitcast.14.owner_ref, s32[24,64]{1,0:T(8,128)} %fusion.4.tiles_ref, f32[1]{0:T(128)S(6)} %add.36.gain_ref, f32[24,8192]{1,0:T(8,128)} %select_convert_fusion.near_ref, bf16[48,8192]{1,0:T(8,128)(2,1)} %slice.6.feat_ref, bf16[48,1024]{1,0:T(8,128)(2,1)} %copy-done.8, ...), custom_call_target="tpu_custom_call" | custom-call | tf_op jit(solution)/shard_map/aggregate/pallas_call | solution.py:155
  68.1 2.9 %collective-permute-start.8 = (bf16[48,2048]{1,0:T(8,128)(2,1)}, bf16[48,2048]{1,0:T(8,128)(2,1)S(1)}, u32[]{:S(2)}, u32[]{:S(2)}) collective-permute-start(bf16[48,2048]{1,0:T(8,128)(2,1)} %aggregate.9), channel_id=1, source_target_pairs={{0,3},{1,2},{2,1},{3,0},{4,7},{5,6},{6,5},{7,4},{8,11},{9,10},{10,... | collective-permute-start | bytes 589832 | tf_op jit(solution)/shard_map/ppermute | solution.py:168
  71.1 4.7 %aggregate.8 = bf16[48,2048]{1,0:T(8,128)(2,1)} custom-call(s32[1]{0:T(128)} %bitcast.10.owner_ref, s32[24,64]{1,0:T(8,128)} %fusion.4.tiles_ref, f32[1]{0:T(128)S(6)} %add.36.gain_ref, f32[24,8192]{1,0:T(8,128)} %select_convert_fusion.near_ref, bf16[48,8192]{1,0:T(8,128)(2,1)} %slice.6.feat_ref, bf16[48,1024]{1,0:T(8,128)(2,1)} %copy-done.8, ...), custom_call_target="tpu_custom_call" | custom-call | tf_op jit(solution)/shard_map/aggregate/pallas_call | solution.py:155
  75.8 0.0 collective-permute-done.9.rest_2_
  75.8 0.4 collective-permute-start.7
  76.2 0.6 stack.35.rows_ref
  76.8 4.8 %aggregate.11.rest_3_ = bf16[48,2048]{1,0:T(8,128)(2,1)} custom-call(s32[1]{0:T(128)} %bitcast.16.owner_ref, s32[24,64]{1,0:T(8,128)} %fusion.4.tiles_ref, f32[1]{0:T(128)S(6)} %add.36.gain_ref, f32[24,8192]{1,0:T(8,128)} %select_convert_fusion.near_ref, bf16[48,8192]{1,0:T(8,128)(2,1)} %slice.6.feat_ref, bf16[48,1024]{1,0:T(8,128)(2,1)} %copy-done.8, ...), custom_call_target="tpu_custom_call" | custom-call | tf_op jit(solution)/shard_map/aggregate/pallas_call | solution.py:155
  81.6 5.7 %aggregate.15.rest_7_ = bf16[80,2048]{1,0:T(8,128)(2,1)} custom-call(s32[1]{0:T(128)} %bitcast.16.owner_ref, s32[24,64]{1,0:T(8,128)} %fusion.4.tiles_ref, f32[1]{0:T(128)S(6)} %add.36.gain_ref, f32[24,8192]{1,0:T(8,128)} %select_convert_fusion.near_ref, bf16[80,8192]{1,0:T(8,128)(2,1)} %slice.7.feat_ref, bf16[80,1024]{1,0:T(8,128)(2,1)} %copy-done, ...), custom_call_target="tpu_custom_call" | custom-call | tf_op jit(solution)/shard_map/aggregate/pallas_call | solution.py:155
  87.3 0.0 collective-permute-done.8.rest_1_
  87.3 15.8 %collective-permute-done.7.rest_0_ = bf16[48,2048]{1,0:T(8,128)(2,1)S(1)} collective-permute-done((bf16[48,2048]{1,0:T(8,128)(2,1)}, bf16[48,2048]{1,0:T(8,128)(2,1)S(1)}, u32[]{:S(2)}, u32[]{:S(2)}) %collective-permute-start.7) | collective-permute-done | bytes 196640 | tf_op jit(solution)/shard_map/ppermute | solution.py:168
  103.1 0.0 collective-permute-done.19.rest_6_
  103.1 0.0 collective-permute-done.18.rest_5_
  103.2 0.0 collective-permute-done.17.rest_4_
  103.2 0.6 copy-done.21
  103.8 0.1 copy-done.16
  103.9 0.1 copy-done.17
  104.1 0.1 copy-done.18
  104.2 8.1 %network.1 = bf16[2048,512]{1,0:T(8,128)(2,1)} custom-call(s32[8]{0:T(128)} %stack.35.rows_ref, bf16[512,512]{1,0:T(8,128)(2,1)} %w_first_ref.1, f32[1,512]{1,0:T(1,128)} %bitcast.19, bf16[512,512]{1,0:T(8,128)(2,1)} %w_second_ref.1, f32[1,512]{1,0:T(1,128)} %bitcast.20, bf16[48,2048]{1,0:T(8,128)(2,1)} %copy-done.21, bf16[48,2048]{1,0:T(8,128)(2,1)} %copy-done.20, ...), custom_call_target="tpu_custom_call" | custom-call | tf_op jit(solution)/shard_map/network/pallas_call | solution.py:174
  (44 shorter events, 0.1 us)
Async XLA Ops:
  0.0 9.4 %copy-start.7 = (bf16[128,8192]{1,0:T(8,128)(2,1)S(1)}, bf16[128,8192]{1,0:T(8,128)(2,1)}, u32[]{:S(2)}) copy-start(bf16[128,8192]{1,0:T(8,128)(2,1)} %param.11) | copy-start | bytes 6291460
  4.5 10.6 %copy-start.25 = (bf16[48,1024]{1,0:T(8,128)(2,1)S(1)}, bf16[48,1024]{1,0:T(8,128)(2,1)}, u32[]{:S(2)}) copy-start(bf16[48,1024]{1,0:T(8,128)(2,1)} %get-tuple-element.24) | copy-start | bytes 294916
  4.5 12.2 %copy-start.24 = (bf16[48,1024]{1,0:T(8,128)(2,1)S(1)}, bf16[48,1024]{1,0:T(8,128)(2,1)}, u32[]{:S(2)}) copy-start(bf16[48,1024]{1,0:T(8,128)(2,1)} %get-tuple-element.25) | copy-start | bytes 294916
  4.5 13.3 %copy-start.15 = (s32[24,8192]{1,0:T(8,128)S(1)}, s32[24,8192]{1,0:T(8,128)}, u32[]{:S(2)}) copy-start(s32[24,8192]{1,0:T(8,128)} %param.15) | copy-start | bytes 2359300
  4.5 13.3 %copy-start.22 = (s32[8192]{0:T(1024)S(1)}, s32[8192]{0:T(1024)}, u32[]{:S(2)}) copy-start(s32[8192]{0:T(1024)} %param.16) | copy-start | bytes 98308
  4.5 8.8 %collective-permute-start = (bf16[48,1024]{1,0:T(8,128)(2,1)}, bf16[48,1024]{1,0:T(8,128)(2,1)S(1)}, u32[]{:S(2)}, u32[]{:S(2)}) collective-permute-start(bf16[48,1024]{1,0:T(8,128)(2,1)} %get-tuple-element.19), channel_id=1, source_target_pairs={{0,4},{4,0},{8,12},{12,8},{16,20},{20,16},{24,28},{28,24},{1,5},{5... | collective-permute-start | bytes 294920 | tf_op jit(solution)/shard_map/ppermute | solution.py:136
  5.1 9.8 %collective-permute-start.1 = (bf16[48,1024]{1,0:T(8,128)(2,1)}, bf16[48,1024]{1,0:T(8,128)(2,1)S(1)}, u32[]{:S(2)}, u32[]{:S(2)}) collective-permute-start(bf16[48,1024]{1,0:T(8,128)(2,1)} %get-tuple-element.20), channel_id=1, source_target_pairs={{0,8},{4,12},{8,0},{12,4},{16,24},{20,28},{24,16},{28,20},{1,9},{5... | collective-permute-start | bytes 294920 | tf_op jit(solution)/shard_map/ppermute | solution.py:136
  7.6 7.5 %collective-permute-start.2 = (bf16[48,1024]{1,0:T(8,128)(2,1)}, bf16[48,1024]{1,0:T(8,128)(2,1)S(1)}, u32[]{:S(2)}, u32[]{:S(2)}) collective-permute-start(bf16[48,1024]{1,0:T(8,128)(2,1)} %get-tuple-element.21), channel_id=1, source_target_pairs={{0,12},{4,8},{8,4},{12,0},{16,28},{20,24},{24,20},{28,16},{1,13},{... | collective-permute-start | bytes 294920 | tf_op jit(solution)/shard_map/ppermute | solution.py:136
  7.7 9.0 %collective-permute-start.3 = (bf16[48,1024]{1,0:T(8,128)(2,1)}, bf16[48,1024]{1,0:T(8,128)(2,1)S(1)}, u32[]{:S(2)}, u32[]{:S(2)}) collective-permute-start(bf16[48,1024]{1,0:T(8,128)(2,1)} %get-tuple-element.22), channel_id=1, source_target_pairs={{0,16},{4,20},{8,24},{12,28},{16,0},{20,4},{24,8},{28,12},{1,17},{... | collective-permute-start | bytes 294920 | tf_op jit(solution)/shard_map/ppermute | solution.py:136
  10.6 17.1 %copy-start.23 = (s32[24,64]{1,0:T(8,128)S(1)}, s32[24,64]{1,0:T(8,128)}, u32[]{:S(2)}) copy-start(s32[24,64]{1,0:T(8,128)} %param.14) | copy-start | bytes 18436
  13.2 12.7 %collective-permute-start.10 = (bf16[80,1024]{1,0:T(8,128)(2,1)}, bf16[80,1024]{1,0:T(8,128)(2,1)S(1)}, u32[]{:S(2)}, u32[]{:S(2)}) collective-permute-start(bf16[80,1024]{1,0:T(8,128)(2,1)} %get-tuple-element.26), channel_id=1, source_target_pairs={{0,4},{4,0},{8,12},{12,8},{16,20},{20,16},{24,28},{28,24},{1,5},{5... | collective-permute-start | bytes 491528 | tf_op jit(solution)/shard_map/ppermute | solution.py:136
  13.3 15.7 %copy-start.8 = (bf16[48,1024]{1,0:T(8,128)(2,1)}, bf16[48,1024]{1,0:T(8,128)(2,1)S(1)}, u32[]{:S(2)}) copy-start(bf16[48,1024]{1,0:T(8,128)(2,1)S(1)} %collective-permute-done.rest_0_) | copy-start | bytes 294916
  13.3 14.3 %collective-permute-start.11 = (bf16[80,1024]{1,0:T(8,128)(2,1)}, bf16[80,1024]{1,0:T(8,128)(2,1)S(1)}, u32[]{:S(2)}, u32[]{:S(2)}) collective-permute-start(bf16[80,1024]{1,0:T(8,128)(2,1)} %get-tuple-element.27), channel_id=1, source_target_pairs={{0,8},{4,12},{8,0},{12,4},{16,24},{20,28},{24,16},{28,20},{1,9},{5... | collective-permute-start | bytes 491528 | tf_op jit(solution)/shard_map/ppermute | solution.py:136
  14.8 14.2 %copy-start.9 = (bf16[48,1024]{1,0:T(8,128)(2,1)}, bf16[48,1024]{1,0:T(8,128)(2,1)S(1)}, u32[]{:S(2)}) copy-start(bf16[48,1024]{1,0:T(8,128)(2,1)S(1)} %collective-permute-done.1.rest_1_) | copy-start | bytes 294916
  14.8 5.6 %collective-permute-start.4 = (bf16[48,1024]{1,0:T(8,128)(2,1)}, bf16[48,1024]{1,0:T(8,128)(2,1)S(1)}, u32[]{:S(2)}, u32[]{:S(2)}) collective-permute-start(bf16[48,1024]{1,0:T(8,128)(2,1)} %get-tuple-element.23), channel_id=1, source_target_pairs={{0,20},{4,16},{8,28},{12,24},{16,4},{20,0},{24,12},{28,8},{1,21},{... | collective-permute-start | bytes 294920 | tf_op jit(solution)/shard_map/ppermute | solution.py:136
  15.1 13.9 %copy-start.10 = (bf16[48,1024]{1,0:T(8,128)(2,1)}, bf16[48,1024]{1,0:T(8,128)(2,1)S(1)}, u32[]{:S(2)}) copy-start(bf16[48,1024]{1,0:T(8,128)(2,1)S(1)} %collective-permute-done.2.rest_2_) | copy-start | bytes 294916
  15.1 7.4 %collective-permute-start.5 = (bf16[48,1024]{1,0:T(8,128)(2,1)S(1)}, bf16[48,1024]{1,0:T(8,128)(2,1)S(1)}, u32[]{:S(2)}, u32[]{:S(2)}) collective-permute-start(bf16[48,1024]{1,0:T(8,128)(2,1)S(1)} %copy-done.25), channel_id=1, source_target_pairs={{0,24},{4,28},{8,16},{12,20},{16,8},{20,12},{24,0},{28,4},{1,25},{... | collective-permute-start | bytes 294920 | tf_op jit(solution)/shard_map/ppermute | solution.py:136
  16.6 12.4 %copy-start.11 = (bf16[48,1024]{1,0:T(8,128)(2,1)}, bf16[48,1024]{1,0:T(8,128)(2,1)S(1)}, u32[]{:S(2)}) copy-start(bf16[48,1024]{1,0:T(8,128)(2,1)S(1)} %collective-permute-done.3.rest_3_) | copy-start | bytes 294916
  16.7 7.5 %collective-permute-start.6 = (bf16[48,1024]{1,0:T(8,128)(2,1)S(1)}, bf16[48,1024]{1,0:T(8,128)(2,1)S(1)}, u32[]{:S(2)}, u32[]{:S(2)}) collective-permute-start(bf16[48,1024]{1,0:T(8,128)(2,1)S(1)} %copy-done.24), channel_id=1, source_target_pairs={{0,28},{4,24},{8,20},{12,16},{16,12},{20,8},{24,4},{28,0},{1,29},{... | collective-permute-start | bytes 294920 | tf_op jit(solution)/shard_map/ppermute | solution.py:136
  20.4 8.7 %copy-start.12 = (bf16[48,1024]{1,0:T(8,128)(2,1)}, bf16[48,1024]{1,0:T(8,128)(2,1)S(1)}, u32[]{:S(2)}) copy-start(bf16[48,1024]{1,0:T(8,128)(2,1)S(1)} %collective-permute-done.4.rest_4_) | copy-start | bytes 294916
  20.4 13.4 %collective-permute-start.12 = (bf16[80,1024]{1,0:T(8,128)(2,1)}, bf16[80,1024]{1,0:T(8,128)(2,1)S(1)}, u32[]{:S(2)}, u32[]{:S(2)}) collective-permute-start(bf16[80,1024]{1,0:T(8,128)(2,1)} %get-tuple-element.28), channel_id=1, source_target_pairs={{0,12},{4,8},{8,4},{12,0},{16,28},{20,24},{24,20},{28,16},{1,13},{... | collective-permute-start | bytes 491528 | tf_op jit(solution)/shard_map/ppermute | solution.py:136
  22.5 6.5 %copy-start.13 = (bf16[48,1024]{1,0:T(8,128)(2,1)}, bf16[48,1024]{1,0:T(8,128)(2,1)S(1)}, u32[]{:S(2)}) copy-start(bf16[48,1024]{1,0:T(8,128)(2,1)S(1)} %collective-permute-done.5.rest_5_) | copy-start | bytes 294916
  22.5 12.8 %collective-permute-start.13 = (bf16[80,1024]{1,0:T(8,128)(2,1)}, bf16[80,1024]{1,0:T(8,128)(2,1)S(1)}, u32[]{:S(2)}, u32[]{:S(2)}) collective-permute-start(bf16[80,1024]{1,0:T(8,128)(2,1)} %get-tuple-element.29), channel_id=1, source_target_pairs={{0,16},{4,20},{8,24},{12,28},{16,0},{20,4},{24,8},{28,12},{1,17},{... | collective-permute-start | bytes 491528 | tf_op jit(solution)/shard_map/ppermute | solution.py:136
  24.2 4.9 %copy-start.14 = (bf16[48,1024]{1,0:T(8,128)(2,1)}, bf16[48,1024]{1,0:T(8,128)(2,1)S(1)}, u32[]{:S(2)}) copy-start(bf16[48,1024]{1,0:T(8,128)(2,1)S(1)} %collective-permute-done.6.rest_6_) | copy-start | bytes 294916
  24.2 16.2 %collective-permute-start.14 = (bf16[80,1024]{1,0:T(8,128)(2,1)}, bf16[80,1024]{1,0:T(8,128)(2,1)S(1)}, u32[]{:S(2)}, u32[]{:S(2)}) collective-permute-start(bf16[80,1024]{1,0:T(8,128)(2,1)} %get-tuple-element.30), channel_id=1, source_target_pairs={{0,20},{4,16},{8,28},{12,24},{16,4},{20,0},{24,12},{28,8},{1,21},{... | collective-permute-start | bytes 491528 | tf_op jit(solution)/shard_map/ppermute | solution.py:136
  25.9 14.5 %copy-start = (bf16[80,1024]{1,0:T(8,128)(2,1)}, bf16[80,1024]{1,0:T(8,128)(2,1)S(1)}, u32[]{:S(2)}) copy-start(bf16[80,1024]{1,0:T(8,128)(2,1)S(1)} %collective-permute-done.10.rest_0_) | copy-start | bytes 491524
  25.9 14.5 %collective-permute-start.15 = (bf16[80,1024]{1,0:T(8,128)(2,1)}, bf16[80,1024]{1,0:T(8,128)(2,1)S(1)}, u32[]{:S(2)}, u32[]{:S(2)}) collective-permute-start(bf16[80,1024]{1,0:T(8,128)(2,1)} %get-tuple-element.31), channel_id=1, source_target_pairs={{0,24},{4,28},{8,16},{12,20},{16,8},{20,12},{24,0},{28,4},{1,25},{... | collective-permute-start | bytes 491528 | tf_op jit(solution)/shard_map/ppermute | solution.py:136
  27.7 12.7 %copy-start.1 = (bf16[80,1024]{1,0:T(8,128)(2,1)}, bf16[80,1024]{1,0:T(8,128)(2,1)S(1)}, u32[]{:S(2)}) copy-start(bf16[80,1024]{1,0:T(8,128)(2,1)S(1)} %collective-permute-done.11.rest_1_) | copy-start | bytes 491524
  27.7 12.7 %collective-permute-start.16 = (bf16[80,1024]{1,0:T(8,128)(2,1)}, bf16[80,1024]{1,0:T(8,128)(2,1)S(1)}, u32[]{:S(2)}, u32[]{:S(2)}) collective-permute-start(bf16[80,1024]{1,0:T(8,128)(2,1)} %get-tuple-element.32), channel_id=1, source_target_pairs={{0,28},{4,24},{8,20},{12,16},{16,12},{20,8},{24,4},{28,0},{1,29},{... | collective-permute-start | bytes 491528 | tf_op jit(solution)/shard_map/ppermute | solution.py:136
  33.8 6.6 %copy-start.2 = (bf16[80,1024]{1,0:T(8,128)(2,1)}, bf16[80,1024]{1,0:T(8,128)(2,1)S(1)}, u32[]{:S(2)}) copy-start(bf16[80,1024]{1,0:T(8,128)(2,1)S(1)} %collective-permute-done.12.rest_2_) | copy-start | bytes 491524
  33.8 42.0 %collective-permute-start.9 = (bf16[48,2048]{1,0:T(8,128)(2,1)}, bf16[48,2048]{1,0:T(8,128)(2,1)S(1)}, u32[]{:S(2)}, u32[]{:S(2)}) collective-permute-start(bf16[48,2048]{1,0:T(8,128)(2,1)} %aggregate.10), channel_id=1, source_target_pairs={{0,1},{1,0},{2,3},{3,2},{4,5},{5,4},{6,7},{7,6},{8,9},{9,8},{10,11... | collective-permute-start | bytes 589832 | tf_op jit(solution)/shard_map/ppermute | solution.py:168
  35.3 5.1 %copy-start.3 = (bf16[80,1024]{1,0:T(8,128)(2,1)}, bf16[80,1024]{1,0:T(8,128)(2,1)S(1)}, u32[]{:S(2)}) copy-start(bf16[80,1024]{1,0:T(8,128)(2,1)S(1)} %collective-permute-done.13.rest_3_) | copy-start | bytes 491524
  40.4 0.7 copy-start.4
  40.4 0.7 copy-start.5
  41.1 0.7 copy-start.6
  47.5 55.6 %collective-permute-start.19 = (bf16[80,2048]{1,0:T(8,128)(2,1)}, bf16[80,2048]{1,0:T(8,128)(2,1)S(1)}, u32[]{:S(2)}, u32[]{:S(2)}) collective-permute-start(bf16[80,2048]{1,0:T(8,128)(2,1)} %aggregate.14), channel_id=1, source_target_pairs={{0,1},{1,0},{2,3},{3,2},{4,5},{5,4},{6,7},{7,6},{8,9},{9,8},{10,11... | collective-permute-start | bytes 983048 | tf_op jit(solution)/shard_map/ppermute | solution.py:168
  55.1 48.1 %collective-permute-start.18 = (bf16[80,2048]{1,0:T(8,128)(2,1)}, bf16[80,2048]{1,0:T(8,128)(2,1)S(1)}, u32[]{:S(2)}, u32[]{:S(2)}) collective-permute-start(bf16[80,2048]{1,0:T(8,128)(2,1)} %aggregate.13), channel_id=1, source_target_pairs={{0,3},{1,2},{2,1},{3,0},{4,7},{5,6},{6,5},{7,4},{8,11},{9,10},{10,... | collective-permute-start | bytes 983048 | tf_op jit(solution)/shard_map/ppermute | solution.py:168
  63.3 39.9 %collective-permute-start.17 = (bf16[80,2048]{1,0:T(8,128)(2,1)}, bf16[80,2048]{1,0:T(8,128)(2,1)S(1)}, u32[]{:S(2)}, u32[]{:S(2)}) collective-permute-start(bf16[80,2048]{1,0:T(8,128)(2,1)} %aggregate.12), channel_id=1, source_target_pairs={{0,2},{1,3},{2,0},{3,1},{4,6},{5,7},{6,4},{7,5},{8,10},{9,11},{10,... | collective-permute-start | bytes 983048 | tf_op jit(solution)/shard_map/ppermute | solution.py:168
  68.1 19.2 %collective-permute-start.8 = (bf16[48,2048]{1,0:T(8,128)(2,1)}, bf16[48,2048]{1,0:T(8,128)(2,1)S(1)}, u32[]{:S(2)}, u32[]{:S(2)}) collective-permute-start(bf16[48,2048]{1,0:T(8,128)(2,1)} %aggregate.9), channel_id=1, source_target_pairs={{0,3},{1,2},{2,1},{3,0},{4,7},{5,6},{6,5},{7,4},{8,11},{9,10},{10,... | collective-permute-start | bytes 589832 | tf_op jit(solution)/shard_map/ppermute | solution.py:168
  75.8 11.5 %copy-start.19 = (bf16[48,2048]{1,0:T(8,128)(2,1)}, bf16[48,2048]{1,0:T(8,128)(2,1)S(1)}, u32[]{:S(2)}) copy-start(bf16[48,2048]{1,0:T(8,128)(2,1)S(1)} %collective-permute-done.9.rest_2_) | copy-start | bytes 589828
  75.8 27.3 %collective-permute-start.7 = (bf16[48,2048]{1,0:T(8,128)(2,1)}, bf16[48,2048]{1,0:T(8,128)(2,1)S(1)}, u32[]{:S(2)}, u32[]{:S(2)}) collective-permute-start(bf16[48,2048]{1,0:T(8,128)(2,1)} %aggregate.8), channel_id=1, source_target_pairs={{0,2},{1,3},{2,0},{3,1},{4,6},{5,7},{6,4},{7,5},{8,10},{9,11},{10,... | collective-permute-start | bytes 589832 | tf_op jit(solution)/shard_map/ppermute | solution.py:168
  87.3 15.8 %copy-start.20 = (bf16[48,2048]{1,0:T(8,128)(2,1)}, bf16[48,2048]{1,0:T(8,128)(2,1)S(1)}, u32[]{:S(2)}) copy-start(bf16[48,2048]{1,0:T(8,128)(2,1)S(1)} %collective-permute-done.8.rest_1_) | copy-start | bytes 589828
  103.1 0.7 copy-start.21
  103.1 0.8 copy-start.16
  103.1 0.9 copy-start.17
  103.2 1.0 copy-start.18
where the time goes:
time: 113 us; the launch traced here: 112 us
  Pallas kernels  55 us (49%)
  waiting for transfers between devices  24.6 us (22%)
  starting transfers between devices  23.8 us (21%)
  local copies, waits for them, and re-layouts  6.44 us (6%)
  other arithmetic  1.62 us (1%)
    pallas_call x8, Pallas kernels, per_device(): pl.pallas_call(functools.partial(gather_kernel, slots=slots), in_specs=[S...  42 us
    ppermute x6, waiting for transfers between devices, per_device(): lax.ppermute(parcels[-1], 'feat', [(k, k ^ shift) for k in range(groups)])  15.8 us
    ppermute x14, starting transfers between devices, per_device(): lax.ppermute(picked[i], 'dom', [(k, k ^ i + 1) for k in range(parts)])  14.6 us
    ppermute x6, starting transfers between devices, per_device(): lax.ppermute(parcels[-1], 'feat', [(k, k ^ shift) for k in range(groups)])  9.24 us
    ppermute x14, waiting for transfers between devices, per_device(): lax.ppermute(picked[i], 'dom', [(k, k ^ i + 1) for k in range(parts)])  8.75 us
    pallas_call x1, Pallas kernels, per_device(): pl.pallas_call(network_kernel, grid=(owned // step,), in_specs=[SMEM, pl....  8.08 us
    pallas_call x2, Pallas kernels, per_device(): pl.pallas_call(functools.partial(pick_kernel, slots=slots), in_specs=[SME...  4.9 us
    slice x2, local copies, waits for them, and re-layouts, per_device(): piece = lax.slice_in_dim(features, low, high, axis=0)  3.39 us
  transfers between devices with their start and end apart: 20, of which 4 were waited for; matrix products, arithmetic and copies ran while one was open for 3% of the time, Pallas kernels for 40%

commit v1 on v0

--- a/solution.py
+++ b/solution.py
@@ -24,26 +24,27 @@
     return (0, first), (first, cols)
 
 
-def pick_kernel(pos_ref, blocks_ref, counts_ref, feat_ref, *out_refs, slots):
+def pick_kernel(pos_ref, blocks_ref, counts_ref, feat_ref, *out_refs, slots, low):
     me = pos_ref[0]
     for i, out_ref in enumerate(out_refs):
         peer = jnp.bitwise_xor(me, i + 1)
         count = counts_ref[peer]
         for s in range(slots):
             start = pl.multiple_of(blocks_ref[peer, s] * BLOCK, BLOCK)
-            tile = feat_ref[:, pl.ds(start, BLOCK)]
+            tile = feat_ref[low : low + out_ref.shape[0], pl.ds(start, BLOCK)]
             out_ref[:, s * BLOCK : (s + 1) * BLOCK] = jnp.where(
                 s < count, tile, jnp.zeros_like(tile)
             )
 
 
-def gather_kernel(owner_ref, tiles_ref, gain_ref, near_ref, feat_ref, *rest, slots):
+def gather_kernel(owner_ref, tiles_ref, gain_ref, near_ref, feat_ref, *rest, slots, low):
     halo_refs, out_ref, table_ref = rest[:-2], rest[-2], rest[-1]
     own = feat_ref.shape[1] // BLOCK
     width = near_ref.shape[0]
     chunk = out_ref.shape[1] // BLOCK
+    high = low + out_ref.shape[0]
     for b in range(own):
-        table_ref[b] = feat_ref[:, b * BLOCK : (b + 1) * BLOCK]
+        table_ref[b] = feat_ref[low:high, b * BLOCK : (b + 1) * BLOCK]
     for i, ref in enumerate(halo_refs):
         for s in range(slots):
             table_ref[own + slots + i * slots + s] = ref[:, s * BLOCK : (s + 1) * BLOCK]
@@ -119,18 +120,16 @@
     own = rows // BLOCK
     owned = rows // groups
 
-    halo, pieces = [], []
+    halo = []
     for low, high in column_parts(cols):
-        piece = lax.slice_in_dim(features, low, high, axis=0)
         picked = pl.pallas_call(
-            functools.partial(pick_kernel, slots=slots),
+            functools.partial(pick_kernel, slots=slots, low=low),
             in_specs=[SMEM, SMEM, SMEM, VMEM],
             out_specs=[VMEM] * (parts - 1),
             out_shape=[jax.ShapeDtypeStruct((high - low, slots * BLOCK), jnp.bfloat16)]
             * (parts - 1),
             name="pick",
-        )(me[None], send_blocks[0], counts[0], piece)
-        pieces.append(piece)
+        )(me[None], send_blocks[0], counts[0], features)
         arrived = []
         for i in range(parts - 1):
             arrived.append(lax.ppermute(picked[i], "dom", [(k, k ^ (i + 1)) for k in range(parts)]))
@@ -147,13 +146,13 @@
     near_rows = jnp.where(entry < degree[None, :], neighbours, -1).astype(jnp.float32)
     parcels, starts = [], []
     for h, (low, high) in enumerate(column_parts(cols)):
-        piece, arrived = pieces[h], halo[h]
+        arrived = halo[h]
         for shift in exchange_order(groups):
             owner = jnp.bitwise_xor(zed, shift)
             at = owner[None]
             parcels.append(
                 pl.pallas_call(
-                    functools.partial(gather_kernel, slots=slots),
+                    functools.partial(gather_kernel, slots=slots, low=low),
                     in_specs=[SMEM, SMEM, SMEM] + [VMEM] * (2 + parts - 1),
                     out_specs=VMEM,
                     out_shape=jax.ShapeDtypeStruct((high - low, owned), jnp.bfloat16),
@@ -161,7 +160,7 @@
                         pltpu.VMEM((own + slots * parts, high - low, BLOCK), jnp.bfloat16)
                     ],
                     name="aggregate",
-                )(at, tiles, gain, near_rows, piece, *arrived)
+                )(at, tiles, gain, near_rows, features, *arrived)
             )
             starts.append(owner * cols + low)
             if shift:

time: 113 us -> 92 us (0.81)
  waiting for transfers between devices: 24.6 us -> 2.34 us
  local copies, waits for them, and re-layouts: 6.44 us -> 2.98 us
  Pallas kernels: 55 us -> 58.3 us
  starting transfers between devices: 23.8 us -> 25.2 us
    ppermute x6, waiting for transfers between devices: 15.8 us -> 0.02 us  [per_device(): lax.ppermute(parcels[-1], 'feat', [(k, k ^ shift) for k in range(groups)])]
    ppermute x14, waiting for transfers between devices: 8.75 us -> 2.32 us  [per_device(): lax.ppermute(picked[i], 'dom', [(k, k ^ i + 1) for k in range(parts)])]
    slice x2 -> x0, local copies, waits for them, and re-layouts: 3.39 us -> none  [per_device(): piece = lax.slice_in_dim(features, low, high, axis=0)]
    pallas_call x10, Pallas kernels: 46.9 us -> 50.2 us  [the longest x8 44.5 us: per_device(): pl.pallas_call(functools.partial(gather_kernel, slots=slots, low=low), in...]
    unnamed x52 -> x50, local copies, waits for them, and re-layouts: 2.44 us -> 2.35 us
  transfers between devices with their start and end apart: 20 -> 20, of which waited for: 4 -> 5; matrix products, arithmetic and copies ran while one was open for 3% -> 2% of each run, Pallas kernels for 40% -> 52%
where the time goes in v1:
time: 92 us; the launch traced here: 91.3 us
  Pallas kernels  58.3 us (63%)
  starting transfers between devices  25.2 us (27%)
  local copies, waits for them, and re-layouts  2.98 us (3%)
  waiting for transfers between devices  2.34 us (3%)
  other arithmetic  1.57 us (2%)
    pallas_call x8, Pallas kernels, per_device(): pl.pallas_call(functools.partial(gather_kernel, slots=slots, low=low), in...  44.5 us
    ppermute x14, starting transfers between devices, per_device(): lax.ppermute(picked[i], 'dom', [(k, k ^ i + 1) for k in range(parts)])  15 us
    ppermute x6, starting transfers between devices, per_device(): lax.ppermute(parcels[-1], 'feat', [(k, k ^ shift) for k in range(groups)])  10.3 us
    pallas_call x1, Pallas kernels, per_device(): pl.pallas_call(network_kernel, grid=(owned // step,), in_specs=[SMEM, pl....  8.07 us
    pallas_call x2, Pallas kernels, per_device(): pl.pallas_call(functools.partial(pick_kernel, slots=slots, low=low), in_s...  5.66 us
    unnamed x50, local copies, waits for them, and re-layouts  2.35 us
    ppermute x14, waiting for transfers between devices, per_device(): lax.ppermute(picked[i], 'dom', [(k, k ^ i + 1) for k in range(parts)])  2.32 us
  transfers between devices with their start and end apart: 20, of which 5 were waited for; matrix products, arithmetic and copies ran while one was open for 2% of the time, Pallas kernels for 52%

profile of v1, /device:TPU:0, one launch (start us, length us, event | category | flops | bytes accessed | tf_op | source)
XLA Modules:
  0.0 91.3 jit_solution(6279989696009626013)
XLA Ops:
  0.0 2.7 %pick.2 = (bf16[48,1024]{1,0:T(8,128)(2,1)}, bf16[48,1024]{1,0:T(8,128)(2,1)}, bf16[48,1024]{1,0:T(8,128)(2,1)}, bf16[48,1024]{1,0:T(8,128)(2,1)}, bf16[48,1024]...) custom-call(s32[1]{0:T(128)} %bitcast.11.pos_ref, s32[8,8]{1,0:T(8,128)} %bitcast.17, s32[8]{0:T(128)} %bitcast.21, ...), custom_call_target="tpu_custom_call" | custom-call | tf_op jit(solution)/shard_map/pick/pallas_call | solution.py:125
  2.8 0.6 collective-permute-start
  3.3 2.6 %collective-permute-start.1 = (bf16[48,1024]{1,0:T(8,128)(2,1)}, bf16[48,1024]{1,0:T(8,128)(2,1)S(1)}, u32[]{:S(2)}, u32[]{:S(2)}) collective-permute-start(bf16[48,1024]{1,0:T(8,128)(2,1)} %get-tuple-element.20), channel_id=1, source_target_pairs={{0,8},{4,12},{8,0},{12,4},{16,24},{20,28},{24,16},{28,20},{1,9},{5... | collective-permute-start | bytes 294920 | tf_op jit(solution)/shard_map/ppermute | solution.py:135
  5.9 0.0 collective-permute-start.2
  5.9 1.8 %collective-permute-start.3 = (bf16[48,1024]{1,0:T(8,128)(2,1)}, bf16[48,1024]{1,0:T(8,128)(2,1)S(1)}, u32[]{:S(2)}, u32[]{:S(2)}) collective-permute-start(bf16[48,1024]{1,0:T(8,128)(2,1)} %get-tuple-element.22), channel_id=1, source_target_pairs={{0,16},{4,20},{8,24},{12,28},{16,0},{20,4},{24,8},{28,12},{1,17},{... | collective-permute-start | bytes 294920 | tf_op jit(solution)/shard_map/ppermute | solution.py:135
  7.7 0.0 collective-permute-start.4
  7.7 2.9 %pick.3 = (bf16[80,1024]{1,0:T(8,128)(2,1)}, bf16[80,1024]{1,0:T(8,128)(2,1)}, bf16[80,1024]{1,0:T(8,128)(2,1)}, bf16[80,1024]{1,0:T(8,128)(2,1)}, bf16[80,1024]...) custom-call(s32[1]{0:T(128)} %bitcast.11.pos_ref, s32[8,8]{1,0:T(8,128)} %bitcast.18, s32[8]{0:T(128)} %bitcast.22, ...), custom_call_target="tpu_custom_call" | custom-call | tf_op jit(solution)/shard_map/pick/pallas_call | solution.py:125
  10.6 0.0 collective-permute-done.rest_0_
  10.6 0.0 copy-done.24
  10.6 2.7 %collective-permute-start.5 = (bf16[48,1024]{1,0:T(8,128)(2,1)S(1)}, bf16[48,1024]{1,0:T(8,128)(2,1)S(1)}, u32[]{:S(2)}, u32[]{:S(2)}) collective-permute-start(bf16[48,1024]{1,0:T(8,128)(2,1)S(1)} %copy-done.24), channel_id=1, source_target_pairs={{0,24},{4,28},{8,16},{12,20},{16,8},{20,12},{24,0},{28,4},{1,25},{... | collective-permute-start | bytes 294920 | tf_op jit(solution)/shard_map/ppermute | solution.py:135
  13.3 0.0 collective-permute-done.1.rest_1_
  13.3 0.1 collective-permute-start.6
  13.5 0.0 collective-permute-done.2.rest_2_
  13.5 0.3 collective-permute-start.10
  13.8 0.0 collective-permute-done.3.rest_3_
  13.8 1.7 %collective-permute-start.11 = (bf16[80,1024]{1,0:T(8,128)(2,1)}, bf16[80,1024]{1,0:T(8,128)(2,1)S(1)}, u32[]{:S(2)}, u32[]{:S(2)}) collective-permute-start(bf16[80,1024]{1,0:T(8,128)(2,1)} %get-tuple-element.27), channel_id=1, source_target_pairs={{0,8},{4,12},{8,0},{12,4},{16,24},{20,28},{24,16},{28,20},{1,9},{5... | collective-permute-start | bytes 491528 | tf_op jit(solution)/shard_map/ppermute | solution.py:135
  15.5 1.0 %select_convert_fusion.near_ref = f32[24,8192]{1,0:T(8,128)} fusion(s32[24,8192]{1,0:T(8,128)S(1)} %copy-done.14, s32[8192]{0:T(1024)S(1)} %copy-done.21), kind=kLoop, calls=%fused_computation | loop fusion | flops 589824 | bytes 1605632 | tf_op jit(solution)/shard_map/convert_element_type | solution.py:146
  16.5 0.0 collective-permute-done.4.rest_4_
  16.5 0.0 collective-permute-start.12
  16.5 0.2 collective-permute-done.5.rest_5_
  16.7 2.2 %collective-permute-start.13 = (bf16[80,1024]{1,0:T(8,128)(2,1)}, bf16[80,1024]{1,0:T(8,128)(2,1)S(1)}, u32[]{:S(2)}, u32[]{:S(2)}) collective-permute-start(bf16[80,1024]{1,0:T(8,128)(2,1)} %get-tuple-element.29), channel_id=1, source_target_pairs={{0,16},{4,20},{8,24},{12,28},{16,0},{20,4},{24,8},{28,12},{1,17},{... | collective-permute-start | bytes 491528 | tf_op jit(solution)/shard_map/ppermute | solution.py:135
  19.0 0.1 collective-permute-done.6.rest_6_
  19.0 1.4 %collective-permute-start.14 = (bf16[80,1024]{1,0:T(8,128)(2,1)}, bf16[80,1024]{1,0:T(8,128)(2,1)S(1)}, u32[]{:S(2)}, u32[]{:S(2)}) collective-permute-start(bf16[80,1024]{1,0:T(8,128)(2,1)} %get-tuple-element.30), channel_id=1, source_target_pairs={{0,20},{4,16},{8,28},{12,24},{16,4},{20,0},{24,12},{28,8},{1,21},{... | collective-permute-start | bytes 491528 | tf_op jit(solution)/shard_map/ppermute | solution.py:135
  20.5 0.0 collective-permute-done.10.rest_0_
  20.5 1.4 %collective-permute-start.15 = (bf16[80,1024]{1,0:T(8,128)(2,1)}, bf16[80,1024]{1,0:T(8,128)(2,1)S(1)}, u32[]{:S(2)}, u32[]{:S(2)}) collective-permute-start(bf16[80,1024]{1,0:T(8,128)(2,1)} %get-tuple-element.31), channel_id=1, source_target_pairs={{0,24},{4,28},{8,16},{12,20},{16,8},{20,12},{24,0},{28,4},{1,25},{... | collective-permute-start | bytes 491528 | tf_op jit(solution)/shard_map/ppermute | solution.py:135
  21.9 1.2 %collective-permute-done.11.rest_1_ = bf16[80,1024]{1,0:T(8,128)(2,1)S(1)} collective-permute-done((bf16[80,1024]{1,0:T(8,128)(2,1)}, bf16[80,1024]{1,0:T(8,128)(2,1)S(1)}, u32[]{:S(2)}, u32[]{:S(2)}) %collective-permute-start.11) | collective-permute-done | bytes 163872 | tf_op jit(solution)/shard_map/ppermute | solution.py:135
  23.1 0.1 collective-permute-start.16
  23.2 0.6 fusion.4.tiles_ref
  24.5 5.2 %aggregate.8 = bf16[48,2048]{1,0:T(8,128)(2,1)} custom-call(s32[1]{0:T(128)} %bitcast.10.owner_ref, s32[24,64]{1,0:T(8,128)} %fusion.4.tiles_ref, f32[1]{0:T(128)S(6)} %add.36.gain_ref, f32[24,8192]{1,0:T(8,128)} %select_convert_fusion.near_ref, bf16[128,8192]{1,0:T(8,128)(2,1)} %feat_ref.19, bf16[48,1024]{1,0:T(8,128)(2,1)} %copy-done.7, ...), custom_call_target="tpu_custom_call" | custom-call | tf_op jit(solution)/shard_map/aggregate/pallas_call | solution.py:154
  29.7 0.0 collective-permute-done.12.rest_2_
  29.7 2.7 %collective-permute-start.7 = (bf16[48,2048]{1,0:T(8,128)(2,1)}, bf16[48,2048]{1,0:T(8,128)(2,1)S(1)}, u32[]{:S(2)}, u32[]{:S(2)}) collective-permute-start(bf16[48,2048]{1,0:T(8,128)(2,1)} %aggregate.8), channel_id=1, source_target_pairs={{0,2},{1,3},{2,0},{3,1},{4,6},{5,7},{6,4},{7,5},{8,10},{9,11},{10,... | collective-permute-start | bytes 589832 | tf_op jit(solution)/shard_map/ppermute | solution.py:167
  32.4 0.0 collective-permute-done.13.rest_3_
  32.4 0.7 collective-permute-done.14.rest_4_
  33.1 0.0 collective-permute-done.15.rest_5_
  33.1 0.1 collective-permute-done.16.rest_6_
  33.2 0.0 copy-done
  33.2 0.6 copy-done.4
  33.8 0.0 copy-done.5
  33.8 0.7 copy-done.6
  34.5 6.0 %aggregate.12 = bf16[80,2048]{1,0:T(8,128)(2,1)} custom-call(s32[1]{0:T(128)} %bitcast.10.owner_ref, s32[24,64]{1,0:T(8,128)} %fusion.4.tiles_ref, f32[1]{0:T(128)S(6)} %add.36.gain_ref, f32[24,8192]{1,0:T(8,128)} %select_convert_fusion.near_ref, bf16[128,8192]{1,0:T(8,128)(2,1)} %feat_ref.19, bf16[80,1024]{1,0:T(8,128)(2,1)} %copy-done, ...), custom_call_target="tpu_custom_call" | custom-call | tf_op jit(solution)/shard_map/aggregate/pallas_call | solution.py:154
  40.5 2.6 %collective-permute-start.17 = (bf16[80,2048]{1,0:T(8,128)(2,1)}, bf16[80,2048]{1,0:T(8,128)(2,1)S(1)}, u32[]{:S(2)}, u32[]{:S(2)}) collective-permute-start(bf16[80,2048]{1,0:T(8,128)(2,1)} %aggregate.12), channel_id=1, source_target_pairs={{0,2},{1,3},{2,0},{3,1},{4,6},{5,7},{6,4},{7,5},{8,10},{9,11},{10,... | collective-permute-start | bytes 983048 | tf_op jit(solution)/shard_map/ppermute | solution.py:167
  43.0 6.0 %aggregate.13 = bf16[80,2048]{1,0:T(8,128)(2,1)} custom-call(s32[1]{0:T(128)} %bitcast.14.owner_ref, s32[24,64]{1,0:T(8,128)} %fusion.4.tiles_ref, f32[1]{0:T(128)S(6)} %add.36.gain_ref, f32[24,8192]{1,0:T(8,128)} %select_convert_fusion.near_ref, bf16[128,8192]{1,0:T(8,128)(2,1)} %feat_ref.19, bf16[80,1024]{1,0:T(8,128)(2,1)} %copy-done, ...), custom_call_target="tpu_custom_call" | custom-call | tf_op jit(solution)/shard_map/aggregate/pallas_call | solution.py:154
  49.0 1.4 %collective-permute-start.18 = (bf16[80,2048]{1,0:T(8,128)(2,1)}, bf16[80,2048]{1,0:T(8,128)(2,1)S(1)}, u32[]{:S(2)}, u32[]{:S(2)}) collective-permute-start(bf16[80,2048]{1,0:T(8,128)(2,1)} %aggregate.13), channel_id=1, source_target_pairs={{0,3},{1,2},{2,1},{3,0},{4,7},{5,6},{6,5},{7,4},{8,11},{9,10},{10,... | collective-permute-start | bytes 983048 | tf_op jit(solution)/shard_map/ppermute | solution.py:167
  50.4 6.0 %aggregate.14 = bf16[80,2048]{1,0:T(8,128)(2,1)} custom-call(s32[1]{0:T(128)} %bitcast.15.owner_ref, s32[24,64]{1,0:T(8,128)} %fusion.4.tiles_ref, f32[1]{0:T(128)S(6)} %add.36.gain_ref, f32[24,8192]{1,0:T(8,128)} %select_convert_fusion.near_ref, bf16[128,8192]{1,0:T(8,128)(2,1)} %feat_ref.19, bf16[80,1024]{1,0:T(8,128)(2,1)} %copy-done, ...), custom_call_target="tpu_custom_call" | custom-call | tf_op jit(solution)/shard_map/aggregate/pallas_call | solution.py:154
  56.4 0.2 collective-permute-start.19
  56.6 5.2 %aggregate.9 = bf16[48,2048]{1,0:T(8,128)(2,1)} custom-call(s32[1]{0:T(128)} %bitcast.14.owner_ref, s32[24,64]{1,0:T(8,128)} %fusion.4.tiles_ref, f32[1]{0:T(128)S(6)} %add.36.gain_ref, f32[24,8192]{1,0:T(8,128)} %select_convert_fusion.near_ref, bf16[128,8192]{1,0:T(8,128)(2,1)} %feat_ref.19, bf16[48,1024]{1,0:T(8,128)(2,1)} %copy-done.7, ...), custom_call_target="tpu_custom_call" | custom-call | tf_op jit(solution)/shard_map/aggregate/pallas_call | solution.py:154
  61.7 2.9 %collective-permute-start.8 = (bf16[48,2048]{1,0:T(8,128)(2,1)}, bf16[48,2048]{1,0:T(8,128)(2,1)S(1)}, u32[]{:S(2)}, u32[]{:S(2)}) collective-permute-start(bf16[48,2048]{1,0:T(8,128)(2,1)} %aggregate.9), channel_id=1, source_target_pairs={{0,3},{1,2},{2,1},{3,0},{4,7},{5,6},{6,5},{7,4},{8,11},{9,10},{10,... | collective-permute-start | bytes 589832 | tf_op jit(solution)/shard_map/ppermute | solution.py:167
  64.7 5.1 %aggregate.10 = bf16[48,2048]{1,0:T(8,128)(2,1)} custom-call(s32[1]{0:T(128)} %bitcast.15.owner_ref, s32[24,64]{1,0:T(8,128)} %fusion.4.tiles_ref, f32[1]{0:T(128)S(6)} %add.36.gain_ref, f32[24,8192]{1,0:T(8,128)} %select_convert_fusion.near_ref, bf16[128,8192]{1,0:T(8,128)(2,1)} %feat_ref.19, bf16[48,1024]{1,0:T(8,128)(2,1)} %copy-done.7, ...), custom_call_target="tpu_custom_call" | custom-call | tf_op jit(solution)/shard_map/aggregate/pallas_call | solution.py:154
  69.8 0.0 collective-permute-done.7.rest_0_
  69.8 0.5 collective-permute-start.9
  70.3 0.6 stack.35.rows_ref
  71.0 5.1 %aggregate.11.rest_3_ = bf16[48,2048]{1,0:T(8,128)(2,1)} custom-call(s32[1]{0:T(128)} %bitcast.16.owner_ref, s32[24,64]{1,0:T(8,128)} %fusion.4.tiles_ref, f32[1]{0:T(128)S(6)} %add.36.gain_ref, f32[24,8192]{1,0:T(8,128)} %select_convert_fusion.near_ref, bf16[128,8192]{1,0:T(8,128)(2,1)} %feat_ref.19, bf16[48,1024]{1,0:T(8,128)(2,1)} %copy-done.7, ...), custom_call_target="tpu_custom_call" | custom-call | tf_op jit(solution)/shard_map/aggregate/pallas_call | solution.py:154
  76.1 6.0 %aggregate.15.rest_7_ = bf16[80,2048]{1,0:T(8,128)(2,1)} custom-call(s32[1]{0:T(128)} %bitcast.16.owner_ref, s32[24,64]{1,0:T(8,128)} %fusion.4.tiles_ref, f32[1]{0:T(128)S(6)} %add.36.gain_ref, f32[24,8192]{1,0:T(8,128)} %select_convert_fusion.near_ref, bf16[128,8192]{1,0:T(8,128)(2,1)} %feat_ref.19, bf16[80,1024]{1,0:T(8,128)(2,1)} %copy-done, ...), custom_call_target="tpu_custom_call" | custom-call | tf_op jit(solution)/shard_map/aggregate/pallas_call | solution.py:154
  82.1 0.0 collective-permute-done.8.rest_1_
  82.1 0.0 collective-permute-done.9.rest_2_
  82.1 0.0 collective-permute-done.17.rest_4_
  82.1 0.0 collective-permute-done.18.rest_5_
  82.2 0.0 collective-permute-done.19.rest_6_
  82.2 0.6 copy-done.19
  82.8 0.1 copy-done.20
  82.9 0.1 copy-done.15
  83.0 0.1 copy-done.16
  83.1 0.1 copy-done.17
  83.2 8.1 %network.1 = bf16[2048,512]{1,0:T(8,128)(2,1)} custom-call(s32[8]{0:T(128)} %stack.35.rows_ref, bf16[512,512]{1,0:T(8,128)(2,1)} %w_first_ref.1, f32[1,512]{1,0:T(1,128)} %bitcast.19, bf16[512,512]{1,0:T(8,128)(2,1)} %w_second_ref.1, f32[1,512]{1,0:T(1,128)} %bitcast.20, bf16[48,2048]{1,0:T(8,128)(2,1)} %copy-done.18, bf16[48,2048]{1,0:T(8,128)(2,1)} %copy-done.19, ...), custom_call_target="tpu_custom_call" | custom-call | tf_op jit(solution)/shard_map/network/pallas_call | solution.py:173
  (40 shorter events, 0.1 us)
Async XLA Ops:
  0.0 15.5 %copy-start.14 = (s32[24,8192]{1,0:T(8,128)S(1)}, s32[24,8192]{1,0:T(8,128)}, u32[]{:S(2)}) copy-start(s32[24,8192]{1,0:T(8,128)} %param.15) | copy-start | bytes 2359300
  0.0 15.5 %copy-start.21 = (s32[8192]{0:T(1024)S(1)}, s32[8192]{0:T(1024)}, u32[]{:S(2)}) copy-start(s32[8192]{0:T(1024)} %param.16) | copy-start | bytes 98308
  2.7 7.9 %copy-start.24 = (bf16[48,1024]{1,0:T(8,128)(2,1)S(1)}, bf16[48,1024]{1,0:T(8,128)(2,1)}, u32[]{:S(2)}) copy-start(bf16[48,1024]{1,0:T(8,128)(2,1)} %get-tuple-element.24) | copy-start | bytes 294916
  2.7 10.6 %copy-start.23 = (bf16[48,1024]{1,0:T(8,128)(2,1)S(1)}, bf16[48,1024]{1,0:T(8,128)(2,1)}, u32[]{:S(2)}) copy-start(bf16[48,1024]{1,0:T(8,128)(2,1)} %get-tuple-element.25) | copy-start | bytes 294916
  2.7 20.5 %copy-start.22 = (s32[24,64]{1,0:T(8,128)S(1)}, s32[24,64]{1,0:T(8,128)}, u32[]{:S(2)}) copy-start(s32[24,64]{1,0:T(8,128)} %param.14) | copy-start | bytes 18436
  2.8 7.9 %collective-permute-start = (bf16[48,1024]{1,0:T(8,128)(2,1)}, bf16[48,1024]{1,0:T(8,128)(2,1)S(1)}, u32[]{:S(2)}, u32[]{:S(2)}) collective-permute-start(bf16[48,1024]{1,0:T(8,128)(2,1)} %get-tuple-element.19), channel_id=1, source_target_pairs={{0,4},{4,0},{8,12},{12,8},{16,20},{20,16},{24,28},{28,24},{1,5},{5... | collective-permute-start | bytes 294920 | tf_op jit(solution)/shard_map/ppermute | solution.py:135
  3.3 10.0 %collective-permute-start.1 = (bf16[48,1024]{1,0:T(8,128)(2,1)}, bf16[48,1024]{1,0:T(8,128)(2,1)S(1)}, u32[]{:S(2)}, u32[]{:S(2)}) collective-permute-start(bf16[48,1024]{1,0:T(8,128)(2,1)} %get-tuple-element.20), channel_id=1, source_target_pairs={{0,8},{4,12},{8,0},{12,4},{16,24},{20,28},{24,16},{28,20},{1,9},{5... | collective-permute-start | bytes 294920 | tf_op jit(solution)/shard_map/ppermute | solution.py:135
  5.9 7.6 %collective-permute-start.2 = (bf16[48,1024]{1,0:T(8,128)(2,1)}, bf16[48,1024]{1,0:T(8,128)(2,1)S(1)}, u32[]{:S(2)}, u32[]{:S(2)}) collective-permute-start(bf16[48,1024]{1,0:T(8,128)(2,1)} %get-tuple-element.21), channel_id=1, source_target_pairs={{0,12},{4,8},{8,4},{12,0},{16,28},{20,24},{24,20},{28,16},{1,13},{... | collective-permute-start | bytes 294920 | tf_op jit(solution)/shard_map/ppermute | solution.py:135
  5.9 7.9 %collective-permute-start.3 = (bf16[48,1024]{1,0:T(8,128)(2,1)}, bf16[48,1024]{1,0:T(8,128)(2,1)S(1)}, u32[]{:S(2)}, u32[]{:S(2)}) collective-permute-start(bf16[48,1024]{1,0:T(8,128)(2,1)} %get-tuple-element.22), channel_id=1, source_target_pairs={{0,16},{4,20},{8,24},{12,28},{16,0},{20,4},{24,8},{28,12},{1,17},{... | collective-permute-start | bytes 294920 | tf_op jit(solution)/shard_map/ppermute | solution.py:135
  7.7 8.8 %collective-permute-start.4 = (bf16[48,1024]{1,0:T(8,128)(2,1)}, bf16[48,1024]{1,0:T(8,128)(2,1)S(1)}, u32[]{:S(2)}, u32[]{:S(2)}) collective-permute-start(bf16[48,1024]{1,0:T(8,128)(2,1)} %get-tuple-element.23), channel_id=1, source_target_pairs={{0,20},{4,16},{8,28},{12,24},{16,4},{20,0},{24,12},{28,8},{1,21},{... | collective-permute-start | bytes 294920 | tf_op jit(solution)/shard_map/ppermute | solution.py:135
  10.6 13.9 %copy-start.7 = (bf16[48,1024]{1,0:T(8,128)(2,1)}, bf16[48,1024]{1,0:T(8,128)(2,1)S(1)}, u32[]{:S(2)}) copy-start(bf16[48,1024]{1,0:T(8,128)(2,1)S(1)} %collective-permute-done.rest_0_) | copy-start | bytes 294916
  10.6 6.1 %collective-permute-start.5 = (bf16[48,1024]{1,0:T(8,128)(2,1)S(1)}, bf16[48,1024]{1,0:T(8,128)(2,1)S(1)}, u32[]{:S(2)}, u32[]{:S(2)}) collective-permute-start(bf16[48,1024]{1,0:T(8,128)(2,1)S(1)} %copy-done.24), channel_id=1, source_target_pairs={{0,24},{4,28},{8,16},{12,20},{16,8},{20,12},{24,0},{28,4},{1,25},{... | collective-permute-start | bytes 294920 | tf_op jit(solution)/shard_map/ppermute | solution.py:135
  13.3 11.2 %copy-start.8 = (bf16[48,1024]{1,0:T(8,128)(2,1)}, bf16[48,1024]{1,0:T(8,128)(2,1)S(1)}, u32[]{:S(2)}) copy-start(bf16[48,1024]{1,0:T(8,128)(2,1)S(1)} %collective-permute-done.1.rest_1_) | copy-start | bytes 294916
  13.3 5.7 %collective-permute-start.6 = (bf16[48,1024]{1,0:T(8,128)(2,1)S(1)}, bf16[48,1024]{1,0:T(8,128)(2,1)S(1)}, u32[]{:S(2)}, u32[]{:S(2)}) collective-permute-start(bf16[48,1024]{1,0:T(8,128)(2,1)S(1)} %copy-done.23), channel_id=1, source_target_pairs={{0,28},{4,24},{8,20},{12,16},{16,12},{20,8},{24,4},{28,0},{1,29},{... | collective-permute-start | bytes 294920 | tf_op jit(solution)/shard_map/ppermute | solution.py:135
  13.5 11.0 %copy-start.9 = (bf16[48,1024]{1,0:T(8,128)(2,1)}, bf16[48,1024]{1,0:T(8,128)(2,1)S(1)}, u32[]{:S(2)}) copy-start(bf16[48,1024]{1,0:T(8,128)(2,1)S(1)} %collective-permute-done.2.rest_2_) | copy-start | bytes 294916
  13.5 7.0 %collective-permute-start.10 = (bf16[80,1024]{1,0:T(8,128)(2,1)}, bf16[80,1024]{1,0:T(8,128)(2,1)S(1)}, u32[]{:S(2)}, u32[]{:S(2)}) collective-permute-start(bf16[80,1024]{1,0:T(8,128)(2,1)} %get-tuple-element.26), channel_id=1, source_target_pairs={{0,4},{4,0},{8,12},{12,8},{16,20},{20,16},{24,28},{28,24},{1,5},{5... | collective-permute-start | bytes 491528 | tf_op jit(solution)/shard_map/ppermute | solution.py:135
  13.8 10.7 %copy-start.10 = (bf16[48,1024]{1,0:T(8,128)(2,1)}, bf16[48,1024]{1,0:T(8,128)(2,1)S(1)}, u32[]{:S(2)}) copy-start(bf16[48,1024]{1,0:T(8,128)(2,1)S(1)} %collective-permute-done.3.rest_3_) | copy-start | bytes 294916
  13.8 9.3 %collective-permute-start.11 = (bf16[80,1024]{1,0:T(8,128)(2,1)}, bf16[80,1024]{1,0:T(8,128)(2,1)S(1)}, u32[]{:S(2)}, u32[]{:S(2)}) collective-permute-start(bf16[80,1024]{1,0:T(8,128)(2,1)} %get-tuple-element.27), channel_id=1, source_target_pairs={{0,8},{4,12},{8,0},{12,4},{16,24},{20,28},{24,16},{28,20},{1,9},{5... | collective-permute-start | bytes 491528 | tf_op jit(solution)/shard_map/ppermute | solution.py:135
  16.5 8.1 %copy-start.11 = (bf16[48,1024]{1,0:T(8,128)(2,1)}, bf16[48,1024]{1,0:T(8,128)(2,1)S(1)}, u32[]{:S(2)}) copy-start(bf16[48,1024]{1,0:T(8,128)(2,1)S(1)} %collective-permute-done.4.rest_4_) | copy-start | bytes 294916
  16.5 13.3 %collective-permute-start.12 = (bf16[80,1024]{1,0:T(8,128)(2,1)}, bf16[80,1024]{1,0:T(8,128)(2,1)S(1)}, u32[]{:S(2)}, u32[]{:S(2)}) collective-permute-start(bf16[80,1024]{1,0:T(8,128)(2,1)} %get-tuple-element.28), channel_id=1, source_target_pairs={{0,12},{4,8},{8,4},{12,0},{16,28},{20,24},{24,20},{28,16},{1,13},{... | collective-permute-start | bytes 491528 | tf_op jit(solution)/shard_map/ppermute | solution.py:135
  16.7 7.8 %copy-start.12 = (bf16[48,1024]{1,0:T(8,128)(2,1)}, bf16[48,1024]{1,0:T(8,128)(2,1)S(1)}, u32[]{:S(2)}) copy-start(bf16[48,1024]{1,0:T(8,128)(2,1)S(1)} %collective-permute-done.5.rest_5_) | copy-start | bytes 294916
  16.7 15.7 %collective-permute-start.13 = (bf16[80,1024]{1,0:T(8,128)(2,1)}, bf16[80,1024]{1,0:T(8,128)(2,1)S(1)}, u32[]{:S(2)}, u32[]{:S(2)}) collective-permute-start(bf16[80,1024]{1,0:T(8,128)(2,1)} %get-tuple-element.29), channel_id=1, source_target_pairs={{0,16},{4,20},{8,24},{12,28},{16,0},{20,4},{24,8},{28,12},{1,17},{... | collective-permute-start | bytes 491528 | tf_op jit(solution)/shard_map/ppermute | solution.py:135
  19.0 5.5 %copy-start.13 = (bf16[48,1024]{1,0:T(8,128)(2,1)}, bf16[48,1024]{1,0:T(8,128)(2,1)S(1)}, u32[]{:S(2)}) copy-start(bf16[48,1024]{1,0:T(8,128)(2,1)S(1)} %collective-permute-done.6.rest_6_) | copy-start | bytes 294916
  19.0 14.1 %collective-permute-start.14 = (bf16[80,1024]{1,0:T(8,128)(2,1)}, bf16[80,1024]{1,0:T(8,128)(2,1)S(1)}, u32[]{:S(2)}, u32[]{:S(2)}) collective-permute-start(bf16[80,1024]{1,0:T(8,128)(2,1)} %get-tuple-element.30), channel_id=1, source_target_pairs={{0,20},{4,16},{8,28},{12,24},{16,4},{20,0},{24,12},{28,8},{1,21},{... | collective-permute-start | bytes 491528 | tf_op jit(solution)/shard_map/ppermute | solution.py:135
  20.5 12.7 %copy-start = (bf16[80,1024]{1,0:T(8,128)(2,1)}, bf16[80,1024]{1,0:T(8,128)(2,1)S(1)}, u32[]{:S(2)}) copy-start(bf16[80,1024]{1,0:T(8,128)(2,1)S(1)} %collective-permute-done.10.rest_0_) | copy-start | bytes 491524
  20.5 12.6 %collective-permute-start.15 = (bf16[80,1024]{1,0:T(8,128)(2,1)}, bf16[80,1024]{1,0:T(8,128)(2,1)S(1)}, u32[]{:S(2)}, u32[]{:S(2)}) collective-permute-start(bf16[80,1024]{1,0:T(8,128)(2,1)} %get-tuple-element.31), channel_id=1, source_target_pairs={{0,24},{4,28},{8,16},{12,20},{16,8},{20,12},{24,0},{28,4},{1,25},{... | collective-permute-start | bytes 491528 | tf_op jit(solution)/shard_map/ppermute | solution.py:135
  23.1 10.1 %copy-start.1 = (bf16[80,1024]{1,0:T(8,128)(2,1)}, bf16[80,1024]{1,0:T(8,128)(2,1)S(1)}, u32[]{:S(2)}) copy-start(bf16[80,1024]{1,0:T(8,128)(2,1)S(1)} %collective-permute-done.11.rest_1_) | copy-start | bytes 491524
  23.1 10.1 %collective-permute-start.16 = (bf16[80,1024]{1,0:T(8,128)(2,1)}, bf16[80,1024]{1,0:T(8,128)(2,1)S(1)}, u32[]{:S(2)}, u32[]{:S(2)}) collective-permute-start(bf16[80,1024]{1,0:T(8,128)(2,1)} %get-tuple-element.32), channel_id=1, source_target_pairs={{0,28},{4,24},{8,20},{12,16},{16,12},{20,8},{24,4},{28,0},{1,29},{... | collective-permute-start | bytes 491528 | tf_op jit(solution)/shard_map/ppermute | solution.py:135
  29.7 3.5 %copy-start.2 = (bf16[80,1024]{1,0:T(8,128)(2,1)}, bf16[80,1024]{1,0:T(8,128)(2,1)S(1)}, u32[]{:S(2)}) copy-start(bf16[80,1024]{1,0:T(8,128)(2,1)S(1)} %collective-permute-done.12.rest_2_) | copy-start | bytes 491524
  29.7 40.1 %collective-permute-start.7 = (bf16[48,2048]{1,0:T(8,128)(2,1)}, bf16[48,2048]{1,0:T(8,128)(2,1)S(1)}, u32[]{:S(2)}, u32[]{:S(2)}) collective-permute-start(bf16[48,2048]{1,0:T(8,128)(2,1)} %aggregate.8), channel_id=1, source_target_pairs={{0,2},{1,3},{2,0},{3,1},{4,6},{5,7},{6,4},{7,5},{8,10},{9,11},{10,... | collective-permute-start | bytes 589832 | tf_op jit(solution)/shard_map/ppermute | solution.py:167
  32.4 0.8 copy-start.3
  33.1 0.7 copy-start.4
  33.1 0.7 copy-start.5
  33.8 0.7 copy-start.6
  40.5 41.7 %collective-permute-start.17 = (bf16[80,2048]{1,0:T(8,128)(2,1)}, bf16[80,2048]{1,0:T(8,128)(2,1)S(1)}, u32[]{:S(2)}, u32[]{:S(2)}) collective-permute-start(bf16[80,2048]{1,0:T(8,128)(2,1)} %aggregate.12), channel_id=1, source_target_pairs={{0,2},{1,3},{2,0},{3,1},{4,6},{5,7},{6,4},{7,5},{8,10},{9,11},{10,... | collective-permute-start | bytes 983048 | tf_op jit(solution)/shard_map/ppermute | solution.py:167
  49.0 33.1 %collective-permute-start.18 = (bf16[80,2048]{1,0:T(8,128)(2,1)}, bf16[80,2048]{1,0:T(8,128)(2,1)S(1)}, u32[]{:S(2)}, u32[]{:S(2)}) collective-permute-start(bf16[80,2048]{1,0:T(8,128)(2,1)} %aggregate.13), channel_id=1, source_target_pairs={{0,3},{1,2},{2,1},{3,0},{4,7},{5,6},{6,5},{7,4},{8,11},{9,10},{10,... | collective-permute-start | bytes 983048 | tf_op jit(solution)/shard_map/ppermute | solution.py:167
  56.4 25.8 %collective-permute-start.19 = (bf16[80,2048]{1,0:T(8,128)(2,1)}, bf16[80,2048]{1,0:T(8,128)(2,1)S(1)}, u32[]{:S(2)}, u32[]{:S(2)}) collective-permute-start(bf16[80,2048]{1,0:T(8,128)(2,1)} %aggregate.14), channel_id=1, source_target_pairs={{0,1},{1,0},{2,3},{3,2},{4,5},{5,4},{6,7},{7,6},{8,9},{9,8},{10,11... | collective-permute-start | bytes 983048 | tf_op jit(solution)/shard_map/ppermute | solution.py:167
  61.7 20.3 %collective-permute-start.8 = (bf16[48,2048]{1,0:T(8,128)(2,1)}, bf16[48,2048]{1,0:T(8,128)(2,1)S(1)}, u32[]{:S(2)}, u32[]{:S(2)}) collective-permute-start(bf16[48,2048]{1,0:T(8,128)(2,1)} %aggregate.9), channel_id=1, source_target_pairs={{0,3},{1,2},{2,1},{3,0},{4,7},{5,6},{6,5},{7,4},{8,11},{9,10},{10,... | collective-permute-start | bytes 589832 | tf_op jit(solution)/shard_map/ppermute | solution.py:167
  69.8 12.3 %copy-start.18 = (bf16[48,2048]{1,0:T(8,128)(2,1)}, bf16[48,2048]{1,0:T(8,128)(2,1)S(1)}, u32[]{:S(2)}) copy-start(bf16[48,2048]{1,0:T(8,128)(2,1)S(1)} %collective-permute-done.7.rest_0_) | copy-start | bytes 589828
  69.8 12.3 %collective-permute-start.9 = (bf16[48,2048]{1,0:T(8,128)(2,1)}, bf16[48,2048]{1,0:T(8,128)(2,1)S(1)}, u32[]{:S(2)}, u32[]{:S(2)}) collective-permute-start(bf16[48,2048]{1,0:T(8,128)(2,1)} %aggregate.10), channel_id=1, source_target_pairs={{0,1},{1,0},{2,3},{3,2},{4,5},{5,4},{6,7},{7,6},{8,9},{9,8},{10,11... | collective-permute-start | bytes 589832 | tf_op jit(solution)/shard_map/ppermute | solution.py:167
  82.1 0.7 copy-start.19
  82.1 0.8 copy-start.20
  82.1 0.8 copy-start.15
  82.1 0.9 copy-start.16
  82.2 1.0 %copy-start.17 = (bf16[80,2048]{1,0:T(8,128)(2,1)}, bf16[80,2048]{1,0:T(8,128)(2,1)S(1)}, u32[]{:S(2)}) copy-start(bf16[80,2048]{1,0:T(8,128)(2,1)S(1)} %collective-permute-done.19.rest_6_) | copy-start | bytes 983044
